TPU v7x, 32 devices: a whole 2x2x4 slice. The times are simulated.
32 devices in a mesh: gx: 2 (over core), gy: 4 (over y, x), gz: 4 (over z).
Axes of the slice: x: 2, y: 2, z: 4, core: 2. Of those that a mesh axis runs over, the one named last changes fastest.
Arguments:
- field: float32 [256, 1024, 512], P('gz', 'gx', 'gy'), may hold values from -48 to 48
- factor_a: float32 [1024, 1024], replicated, may hold values from -0.5 to 3.5
- factor_b: float32 [512, 512], replicated, may hold values from -0.5 to 3.5
- factor_c: float32 [256, 256], replicated, may hold values from -0.5 to 3.5
Outputs:
- propagated: float32 [256, 1024, 512], P('gz', 'gx', 'gy')
All inputs are finite; a program needn't handle non-finite values.
Results may differ from a plain program's by a relative error of at most 0.00007.
Values sent between devices are 32-bit elements; how exact they have to be, the bound alone decides.
A program may use at most 192 MiB of HBM per device.

v0:
```python
import functools

import jax
import jax.numpy as jnp
from jax import lax
from jax.experimental import pallas as pl
from jax.experimental.pallas import tpu as pltpu
from jax.sharding import PartitionSpec as P

epsilon = 1e-06
target_ratio = 0.5
slots = 4
ring = 8
hold = 3
late = 2
F32 = jnp.float32
MESH = pl.DeviceIdType.MESH


def halves(x):
    top = lax.reduce_precision(x, 8, 7)
    return jnp.stack([top.astype(jnp.bfloat16), (x - top).astype(jnp.bfloat16)])


def split(x):
    top = x.astype(jnp.bfloat16)
    return top, (x - top.astype(F32)).astype(jnp.bfloat16)


def dot(a, b):
    return jnp.dot(a, b, preferred_element_type=F32)


def left_dot(matrix, x):
    top, low = split(x)
    return dot(matrix[0], top) + dot(matrix[1], top) + dot(matrix[0], low)


def right_dot(x, matrix):
    top, low = split(x)
    return dot(top, matrix[0]) + dot(top, matrix[1]) + dot(low, matrix[0])


def squares(x):
    return jnp.sum((x * x).reshape(-1, 8, x.shape[-1]), axis=0)


def pipeline_kernel(
    counts,
    chunk,
    field,
    matrix_a,
    matrix_b,
    matrix_c,
    first,
    mixed,
    twice,
    planes,
    far_field,
    far_mixed,
    sums,
    line,
    made,
    arrived,
    product,
    form,
    mode_a,
    made_a,
    line_send,
    line_recv,
    line_own,
    credit,
    back_send,
    back_recv,
    back_own,
    plane_send,
    plane_recv,
    plane_own,
    home_send,
    home_recv,
    home_own,
    far_send,
    far_recv,
    mixed_send,
    mixed_recv,
    local,
):
    count_x, count_y, count_z = counts
    me_x, me_y, me_z = (lax.axis_index(a) for a in ("gx", "gy", "gz"))
    depth, rows, width = field.shape
    share = depth // count_y
    chunks = rows // chunk
    wide = 2 * chunk
    steps = chunks // 2

    half = count_z // 2
    hub = half - 1
    in_left = me_z < half
    place = jnp.where(in_left, me_z, count_z - 1 - me_z)
    near_hub = jnp.where(in_left, hub, count_z - 1 - hub)
    far_hub = jnp.where(in_left, count_z - 1 - hub, hub)
    is_hub = place == hub

    def seat(m, near):
        return jnp.where(in_left == near, m, count_z - 1 - m) if near else jnp.where(in_left, count_z - 1 - m, m)

    def lines(c, size):
        return pl.ds(pl.multiple_of(c * size, size), size)

    def peer(me, s, count):
        return lax.rem(me + s, count)

    def remote(src, dst, send, recv, axis, to):
        return pltpu.make_async_remote_copy(
            src_ref=src, dst_ref=dst, send_sem=send, recv_sem=recv, device_id={axis: to}, device_id_type=MESH
        )

    barrier = pltpu.get_barrier_semaphore()
    for axis, me, count in (("gx", me_x, count_x), ("gy", me_y, count_y), ("gz", me_z, count_z)):
        for s in range(1, count):
            pl.semaphore_signal(barrier, inc=1, device_id={axis: peer(me, s, count)}, device_id_type=MESH)
    pl.semaphore_wait(barrier, count_x + count_y + count_z - 3)

    def line_far(c):
        return remote(
            field.at[:, lines(c, chunk), :],
            line.at[c % slots, half + place],
            line_send.at[c % slots, 1],
            line_recv.at[c % slots, half + place],
            "gz",
            far_hub,
        )

    def line_near(c):
        return remote(
            field.at[:, lines(c, chunk), :],
            line.at[c % slots, 1 + place],
            line_send.at[c % slots, 0],
            line_recv.at[c % slots, 1 + place],
            "gz",
            near_hub,
        )

    def line_local(c):
        return pltpu.make_async_copy(
            field.at[:, lines(c, chunk), :], line.at[c % slots, 0], line_own.at[c % slots]
        )

    def line_start(c, first_time):
        if not first_time:
            pl.semaphore_wait(credit.at[1], 1)
            line_far(c - slots).wait_send()
        line_far(c).start()

        @pl.when(is_hub)
        def _():
            line_local(c).start()

        if hub > 0:

            @pl.when(jnp.logical_not(is_hub))
            def _():
                if not first_time:
                    pl.semaphore_wait(credit.at[0], 1)
                    line_near(c - slots).wait_send()
                line_near(c).start()

    def line_finish(c):
        line_far(c).wait_send()
        if hub > 0:

            @pl.when(jnp.logical_not(is_hub))
            def _():
                line_near(c).wait_send()

    def back_copy(c, m, e):
        return remote(
            made.at[c % slots, 2 + 2 * m + e],
            (mixed, twice)[e].at[:, lines(c, chunk), :],
            back_send.at[c % slots, m, e],
            back_recv.at[c % ring, e],
            "gz",
            seat(m, True),
        )

    def back_local(c, e):
        return pltpu.make_async_copy(
            made.at[c % slots, e], (mixed, twice)[e].at[:, lines(c, chunk), :], back_own.at[c % slots, e]
        )

    def back_wait(c, e):
        @pl.when(is_hub)
        def _():
            back_local(c, e).wait()
            for m in range(hub):
                back_copy(c, m, e).wait_send()

        if hub > 0:

            @pl.when(jnp.logical_not(is_hub))
            def _():
                back_copy(c, 0, e).wait_recv()

    def line_product(c):
        slot = c % slots
        line_local(c).wait()
        for q in range(1, count_z):
            remote(
                field.at[:, lines(c, chunk), :],
                line.at[slot, q],
                line_send.at[slot, 1],
                line_recv.at[slot, q],
                "gz",
                far_hub,
            ).wait_recv()
        outs = 2 * half
        flat = line.reshape(slots, count_z, depth * chunk, width)
        flat_made = made.reshape(slots, outs, depth * chunk, width)
        for i in range(0, chunk, 2):
            x = jnp.concatenate(
                [
                    jnp.concatenate(
                        [flat[slot, q, pl.ds(i + e, depth, stride=chunk), :] for q in range(count_z)], axis=0
                    )
                    for e in range(2)
                ],
                axis=1,
            )
            y = left_dot(matrix_c, x)
            for r in range(outs):
                for e in range(2):
                    flat_made[slot, r, pl.ds(i + e, depth, stride=chunk), :] = y[
                        r * depth : (r + 1) * depth, e * width : (e + 1) * width
                    ]
        for e in range(2):
            for m in range(hub):
                back_copy(c, m, e).start()
            back_local(c, e).start()

        @pl.when(c + slots < chunks)
        def _():
            for m in range(hub):
                pl.semaphore_signal(credit.at[0], inc=1, device_id={"gz": seat(m, True)}, device_id_type=MESH)
            for m in range(half):
                pl.semaphore_signal(credit.at[1], inc=1, device_id={"gz": seat(m, False)}, device_id_type=MESH)

    def quarter(q):
        return pl.ds(q * share, share)

    def plane_copy(src, c, tick, s):
        to = peer(me_y, s, count_y)
        return remote(
            src.at[quarter(to), lines(c, wide), :],
            arrived.at[me_y, :, lines(c, wide), :],
            plane_send.at[tick % ring, s],
            plane_recv.at[tick % ring, s],
            "gy",
            to,
        )

    def plane_local(src, c, tick):
        return pltpu.make_async_copy(
            src.at[quarter(me_y), lines(c, wide), :],
            arrived.at[me_y, :, lines(c, wide), :],
            plane_own.at[tick % ring],
        )

    def plane_start(src, c, tick):
        for s in range(1, count_y):
            plane_copy(src, c, tick, s).start()
        plane_local(src, c, tick).start()

    def home_copy(phase, c, tick, s):
        to = peer(me_y, s, count_y)
        return remote(
            product.at[tick % hold, to],
            planes.at[phase, quarter(me_y), lines(c, wide), :],
            home_send.at[tick % ring, s],
            home_recv.at[tick % ring, s],
            "gy",
            to,
        )

    def home_local(phase, c, tick):
        return pltpu.make_async_copy(
            product.at[tick % hold, me_y],
            planes.at[phase, quarter(me_y), lines(c, wide), :],
            home_own.at[tick % ring],
        )

    def plane_product(phase, c, tick):
        plane_local(field, c, tick).wait()
        for s in range(1, count_y):
            plane_copy(field, c, tick, s).wait()
        x = jnp.concatenate(
            [arrived[q, :, lines(c, wide), :].reshape(share * wide, width) for q in range(count_y)], axis=1
        )
        y = right_dot(x, matrix_b)
        for q in range(count_y):
            product[tick % hold, q] = y[:, q * width : (q + 1) * width].reshape(share, wide, width)
        for s in range(1, count_y):
            home_copy(phase, c, tick, s).start()
        home_local(phase, c, tick).start()

    def home_wait(phase, c, tick):
        home_local(phase, c, tick).wait()
        for s in range(1, count_y):
            home_copy(phase, c, tick, s).wait()

    def far_copy(s):
        return remote(
            field, far_field.at[s - 1], far_send.at[s - 1], far_recv.at[s - 1], "gx", peer(me_x, s, count_x)
        )

    def far_mixed_copy(c, s):
        return remote(
            mixed.at[:, lines(c, wide), :],
            far_mixed.at[s - 1, :, lines(c, wide), :],
            mixed_send.at[c, s - 1],
            mixed_recv.at[c, s - 1],
            "gx",
            peer(me_x, s, count_x),
        )

    def mode_one_pair(k):
        pair = pl.ds(2 * k, 2)
        loads = [pltpu.make_async_copy(field.at[pair], mode_a.at[0], local.at[0])]
        for s in range(1, count_x):
            loads.append(pltpu.make_async_copy(far_field.at[s - 1, pair], mode_a.at[s], local.at[s]))
        for load in loads:
            load.start()
        for load in loads:
            load.wait()
        sums[0] += squares(mode_a[0])
        x = jnp.concatenate(
            [jnp.concatenate([mode_a[s, e] for s in range(count_x)], axis=0) for e in range(2)], axis=1
        )
        y = left_dot(matrix_a, x)
        for e in range(2):
            made_a[e] = y[:, e * width : (e + 1) * width]
        store = pltpu.make_async_copy(made_a, first.at[pair], local.at[0])
        store.start()
        store.wait()

    def mix(c):
        here = lines(c, wide)
        refs = (first.at[:, here, :], mixed.at[:, here, :], planes.at[0, :, here, :])
        loads = [pltpu.make_async_copy(ref, form.at[e], local.at[e]) for e, ref in enumerate(refs)]
        for load in loads:
            load.start()
        for load in loads:
            load.wait()

        def body(k, total):
            once = form[1, k]
            value = form[0, k] + form[2, k] + once
            form[0, k] = value
            form[1, k] = value + once
            return total + squares(value)

        sums[1] += lax.fori_loop(0, depth, body, jnp.zeros((8, width), F32))
        stores = [pltpu.make_async_copy(form.at[e], refs[e], local.at[e]) for e in range(2)]
        for store in stores:
            store.start()
        for store in stores:
            store.wait()

    for c in range(slots):
        line_start(c, True)
    for s in range(1, count_x):
        far_copy(s).start()
    sums[...] = jnp.zeros_like(sums)

    pairs = depth // 2
    each = pl.cdiv(pairs, steps)

    def valid(tick):
        return ((tick >= 0) & (tick < steps)) | ((tick >= steps + late) & (tick < chunks + late))

    def phase_of(tick):
        return jnp.where(tick < steps, 0, 1)

    def chunk_of(tick):
        return jnp.where(tick < steps, tick, tick - steps - late)

    def tick_body(t, carry):
        @pl.when((t >= late) & (t < chunks + late))
        def _():
            back_wait(t - late, 0)

        @pl.when((t >= slots) & (t < chunks + slots))
        def _():
            back_wait(t - slots, 1)

        @pl.when((t < chunks) & is_hub)
        def _():
            line_product(t)

        @pl.when(t + slots < chunks)
        def _():
            line_start(t + slots, False)

        @pl.when(t < steps)
        def _():
            plane_start(field, t, t)

        @pl.when((t >= steps + late) & (t < chunks + late))
        def _():
            c = t - steps - late
            mix(c)
            plane_start(mixed, c, t)
            for s in range(1, count_x):
                far_mixed_copy(c, s).start()

        ready = t - 4

        @pl.when(valid(ready))
        def _():
            home_wait(phase_of(ready), chunk_of(ready), ready)

        come = t - 2

        @pl.when(valid(come))
        def _():
            plane_product(phase_of(come), chunk_of(come), come)

        @pl.when(t == 1)
        def _():
            for s in range(1, count_x):
                far_copy(s).wait()

        @pl.when((t >= 1) & (t <= steps))
        def _():
            def one(i, carry):
                k = (t - 1) * each + i

                @pl.when(k < pairs)
                def _():
                    mode_one_pair(k)

                return carry

            lax.fori_loop(0, each, one, 0)

        return carry

    lax.fori_loop(0, chunks + late + 4, tick_body, 0)
    for c in range(chunks - slots, chunks):
        line_finish(c)

    def last(c, carry):
        for s in range(1, count_x):
            far_mixed_copy(c, s).wait()
        return carry

    lax.fori_loop(0, steps, last, 0)


def pipeline(field, matrix_a, matrix_b, matrix_c, counts, chunk):
    count_x, count_y, count_z = counts
    depth, rows, width = field.shape
    share = depth // count_y
    steps = rows // chunk // 2
    wide = 2 * chunk
    half = count_z // 2
    anywhere = pl.BlockSpec(memory_space=pl.ANY)
    vmem = pl.BlockSpec(memory_space=pltpu.VMEM)
    block = jax.ShapeDtypeStruct((depth, rows, width), F32)
    far = jax.ShapeDtypeStruct((count_x - 1, depth, rows, width), F32)
    dma = pltpu.SemaphoreType.DMA
    scratch = [
        pltpu.VMEM((slots, count_z, depth, chunk, width), F32),
        pltpu.VMEM((slots, 2 * half, depth, chunk, width), F32),
        pltpu.VMEM((count_y, share, rows, width), F32),
        pltpu.VMEM((hold, count_y, share, wide, width), F32),
        pltpu.VMEM((3, depth, wide, width), F32),
        pltpu.VMEM((count_x, 2, rows, width), F32),
        pltpu.VMEM((2, rows, width), F32),
        dma((slots, 2)),
        dma((slots, count_z)),
        dma((slots,)),
        pltpu.SemaphoreType.REGULAR((2,)),
        dma((slots, max(half - 1, 1), 2)),
        dma((ring, 2)),
        dma((slots, 2)),
        dma((ring, count_y)),
        dma((ring, count_y)),
        dma((ring,)),
        dma((ring, count_y)),
        dma((ring, count_y)),
        dma((ring,)),
        dma((count_x - 1,)),
        dma((count_x - 1,)),
        dma((steps, count_x - 1)),
        dma((steps, count_x - 1)),
        dma((max(count_x, 3),)),
    ]
    return pl.pallas_call(
        functools.partial(pipeline_kernel, counts, chunk),
        in_specs=[anywhere, vmem, vmem, vmem],
        out_specs=[anywhere] * 6 + [vmem],
        out_shape=[
            block,
            block,
            block,
            jax.ShapeDtypeStruct((2, depth, rows, width), F32),
            far,
            far,
            jax.ShapeDtypeStruct((2, 8, width), F32),
        ],
        scratch_shapes=scratch,
        compiler_params=pltpu.CompilerParams(
            collective_id=0, has_side_effects=True, vmem_limit_bytes=64 * 1024 * 1024 - 65536
        ),
        name="pipeline",
    )(field, matrix_a, matrix_b, matrix_c)


def finish_kernel(parts, step, matrix, *refs):
    blocks = refs[:parts]
    planes, twice, field, first, out = refs[parts:]
    pair, rows, width = out.shape
    x = jnp.concatenate(
        [jnp.concatenate([block[k] for block in blocks], axis=0) for k in range(pair)], axis=1
    )
    y = left_dot(matrix, x)
    one = step[0]
    two = one * one / 2.0
    for k in range(pair):
        second = y[:, k * width : (k + 1) * width] + planes[k] + twice[k]
        out[k] = field[k] - one * first[k] + two * second


def finish(step, matrix, mixed, far_mixed, planes, twice, field, first):
    depth, rows, width = field.shape
    count = far_mixed.shape[0]
    pair = 2
    block = pl.BlockSpec((pair, rows, width), lambda k: (k, 0, 0))

    def of(s):
        return pl.BlockSpec((None, pair, rows, width), lambda k: (s, k, 0, 0))

    return pl.pallas_call(
        functools.partial(finish_kernel, 1 + count),
        grid=(depth // pair,),
        in_specs=[
            pl.BlockSpec(memory_space=pltpu.SMEM),
            pl.BlockSpec(matrix.shape, lambda k: (0, 0, 0)),
            block,
            *[of(s) for s in range(count)],
            of(1),
            block,
            block,
            block,
        ],
        out_specs=block,
        out_shape=jax.ShapeDtypeStruct(field.shape, F32),
        name="finish",
    )(step, matrix, mixed, *[far_mixed] * count, planes, twice, field, first)


def line_matrix(factor, count, depth, me):
    half = count // 2
    hub = half - 1
    squared = jnp.dot(factor, factor, precision=lax.Precision.HIGHEST)

    def block(matrix, i, j):
        return matrix[i * depth : (i + 1) * depth, j * depth : (j + 1) * depth]

    def side(mine, theirs):
        return jnp.block(
            [
                [block(matrix, mine[m], w) for w in [mine[hub]] + mine[:hub] + theirs]
                for m in [hub] + list(range(hub))
                for matrix in (factor, squared)
            ]
        )

    left = list(range(half))
    right = list(range(count - 1, half - 1, -1))
    return jnp.where(me < half, side(left, right), side(right, left))


def on_device(field, factor_a, factor_b, factor_c):
    counts = tuple(lax.axis_size(a) for a in ("gx", "gy", "gz"))
    count_x, count_y, count_z = counts
    me_x, me_z = lax.axis_index("gx"), lax.axis_index("gz")
    depth, rows, width = field.shape

    rows_a = lax.dynamic_slice_in_dim(factor_a, me_x * rows, rows, 0)
    matrix_a = jnp.concatenate(
        [
            lax.dynamic_slice_in_dim(rows_a, lax.rem(me_x + count_x - s, count_x) * rows, rows, 1)
            for s in range(count_x)
        ],
        axis=1,
    )

    matrix_c = line_matrix(factor_c, count_z, depth, me_z)
    matrix_a, matrix_b, matrix_c = halves(matrix_a), halves(factor_b.T), halves(matrix_c)

    chunk = min(16, rows // 2)
    first, mixed, twice, planes, _, far_mixed, sums = pipeline(field, matrix_a, matrix_b, matrix_c, counts, chunk)
    sizes = lax.psum(jnp.sum(sums, axis=(1, 2)), ("gx", "gy", "gz"))
    step = target_ratio * jnp.sqrt(sizes[0] / (sizes[1] + epsilon))
    return finish(step[None], matrix_a, mixed, far_mixed, planes, twice, field, first)


def solution(mesh):
    return jax.shard_map(
        on_device,
        mesh=mesh,
        in_specs=(P("gz", "gx", "gy"), P(), P(), P()),
        out_specs=P("gz", "gx", "gy"),
        check_vma=False,
    )
```

profile of v0, /device:TPU:0, one launch (start us, length us, event | category | flops | bytes accessed | tf_op | source)
XLA Modules:
  0.0 935.1 jit_solution(6375509037399508128)
XLA Ops:
  0.0 0.0 copy-start.1
  0.0 1.5 fusion.10
  1.5 0.1 fusion.8
  1.6 1.2 fusion.7
  2.8 0.3 fusion.6
  3.1 0.7 pad_maximum_fusion.3.matrix_c
  3.9 0.0 copy-done.1
  3.9 0.3 copy.5
  4.2 0.0 copy-start
  4.2 0.2 fusion.3
  4.4 1.1 pad_maximum_fusion.2.matrix_b
  5.5 1.3 copy-done
  6.8 0.6 dynamic-slice_bitcast_fusion.1
  7.4 0.4 reduce-precision_convert_fusion
  7.8 1.5 pad_maximum_fusion.1.matrix_a.matrix
  9.3 830.0 %pipeline.1 = (f32[64,512,128]{2,1,0:T(8,128)}, f32[64,512,128]{2,1,0:T(8,128)}, f32[64,512,128]{2,1,0:T(8,128)}, f32[2,64,512,128]{3,2,1,0:T(8,128)}, f32[1,64,...) custom-call(f32[64,512,128]{2,1,0:T(8,128)} %refs_4_.1, ...), custom_call_target="tpu_custom_call" | custom-call | tf_op jit(solution)/shard_map/pipeline/pallas_call | solution.py:498
  839.3 0.8 reduce_sum.9
  840.1 39.6 %psum.7 = f32[2]{0:T(128)S(1)} all-reduce(f32[2]{0:T(128)S(1)} %reduce_sum.9), channel_id=1, replica_groups=mesh['gx'=2,'gy'=4,'gz'=4] {'gx','gy','gz'}, use_global_device_ids=true, to_apply=%region_1.3 | all-reduce | flops 2 | bytes 16 | tf_op jit(solution)/shard_map/psum | solution.py:604
  879.7 0.6 fusion.9
  881.6 53.5 %finish.1 = f32[64,512,128]{2,1,0:T(8,128)} custom-call(f32[1]{0:T(128)S(6)} %mul_shard_map.4.step, bf16[2,512,1024]{2,1,0:T(8,128)(2,1)} %pad_maximum_fusion.1.matrix_a.matrix, f32[64,512,128]{2,1,0:T(8,128)} %get-tuple-element.13.refs_0_, f32[1,64,512,128]{3,2,1,0:T(8,128)} %get-tuple-element.14.refs_1_, f32[2,64,512,128]{3,2,1,0:T(8,128)} %get-tuple-element.15.refs_2_, ...), custom_call_target="tpu_custom_call" | custom-call | tf_op jit(solution)/shard_map/finish/pallas_call | solution.py:543
  (1 shorter events, 0.0 us)
Async XLA Ops:
  0.0 3.9 copy-start.1
  4.2 2.6 copy-start
where the time goes:
time: 937 us; the launch traced here: 935 us
  Pallas kernels  884 us (94%)
  blocking collectives  39.6 us (4%)
    pallas_call x1, Pallas kernels, pipeline(): pl.pallas_call(functools.partial(pipeline_kernel, counts, chunk), in_spec...  830 us
    pallas_call x1, Pallas kernels, finish(): pl.pallas_call(functools.partial(finish_kernel, 1 + count), grid=(depth /...  53.5 us
    psum x1, blocking collectives, on_device(): sizes = lax.psum(jnp.sum(sums, axis=(1, 2)), ('gx', 'gy', 'gz'))  39.6 us

commit v1 on v0

--- a/solution.py
+++ b/solution.py
@@ -12,7 +12,7 @@
 slots = 4
 ring = 8
 hold = 3
-late = 2
+late = 1
 F32 = jnp.float32
 MESH = pl.DeviceIdType.MESH
 
@@ -84,6 +84,9 @@
     mixed_send,
     mixed_recv,
     local,
+    gathered,
+    sums_send,
+    sums_recv,
 ):
     count_x, count_y, count_z = counts
     me_x, me_y, me_z = (lax.axis_index(a) for a in ("gx", "gy", "gz"))
@@ -372,18 +375,46 @@
     sums[...] = jnp.zeros_like(sums)
 
     pairs = depth // 2
-    each = pl.cdiv(pairs, steps)
+    each = pl.cdiv(pairs, steps - 1)
 
     def valid(tick):
-        return ((tick >= 0) & (tick < steps)) | ((tick >= steps + late) & (tick < chunks + late))
+        return ((tick >= 0) & (tick < chunks - 1)) | (tick == chunks - 1 + late)
 
     def phase_of(tick):
         return jnp.where(tick < steps, 0, 1)
 
     def chunk_of(tick):
-        return jnp.where(tick < steps, tick, tick - steps - late)
+        return jnp.where(tick < steps, tick, jnp.minimum(tick - steps, steps - 1))
+
+    axes = (("gx", me_x, count_x), ("gy", me_y, count_y), ("gz", me_z, count_z))
+
+    def sums_copy(a, s):
+        axis, me, count = axes[a]
+        return remote(
+            sums, gathered.at[a, me], sums_send.at[a, s], sums_recv.at[a, s], axis, peer(me, s, count)
+        )
+
+    def sums_start(a):
+        for s in range(1, axes[a][2]):
+            sums_copy(a, s).start()
+
+    def sums_finish(a):
+        axis, me, count = axes[a]
+        for s in range(1, count):
+            sums_copy(a, s).wait()
+        gathered[a, me] = sums[...]
+        total = gathered[a, 0]
+        for q in range(1, count):
+            total = total + gathered[a, q]
+        sums[...] = total
 
     def tick_body(t, carry):
+        for a in range(3):
+
+            @pl.when(t == chunks + late + a)
+            def _():
+                sums_finish(a)
+
         @pl.when((t >= late) & (t < chunks + late))
         def _():
             back_wait(t - late, 0)
@@ -404,20 +435,20 @@
         def _():
             plane_start(field, t, t)
 
-        @pl.when((t >= steps + late) & (t < chunks + late))
-        def _():
-            c = t - steps - late
+        ready = t - 4
+
+        @pl.when(valid(ready))
+        def _():
+            home_wait(phase_of(ready), chunk_of(ready), ready)
+
+        @pl.when((t >= steps) & valid(t))
+        def _():
+            c = chunk_of(t)
             mix(c)
             plane_start(mixed, c, t)
             for s in range(1, count_x):
                 far_mixed_copy(c, s).start()
 
-        ready = t - 4
-
-        @pl.when(valid(ready))
-        def _():
-            home_wait(phase_of(ready), chunk_of(ready), ready)
-
         come = t - 2
 
         @pl.when(valid(come))
@@ -429,7 +460,7 @@
             for s in range(1, count_x):
                 far_copy(s).wait()
 
-        @pl.when((t >= 1) & (t <= steps))
+        @pl.when((t >= 1) & (t < steps))
         def _():
             def one(i, carry):
                 k = (t - 1) * each + i
@@ -441,6 +472,12 @@
                 return carry
 
             lax.fori_loop(0, each, one, 0)
+
+        for a in range(3):
+
+            @pl.when(t == chunks - 1 + late + a)
+            def _():
+                sums_start(a)
 
         return carry
 
@@ -494,6 +531,9 @@
         dma((steps, count_x - 1)),
         dma((steps, count_x - 1)),
         dma((max(count_x, 3),)),
+        pltpu.VMEM((3, max(counts), 2, 8, width), F32),
+        dma((3, max(counts))),
+        dma((3, max(counts))),
     ]
     return pl.pallas_call(
         functools.partial(pipeline_kernel, counts, chunk),
@@ -599,9 +639,9 @@
     matrix_c = line_matrix(factor_c, count_z, depth, me_z)
     matrix_a, matrix_b, matrix_c = halves(matrix_a), halves(factor_b.T), halves(matrix_c)
 
-    chunk = min(16, rows // 2)
+    chunk = min(16, rows // 4)
     first, mixed, twice, planes, _, far_mixed, sums = pipeline(field, matrix_a, matrix_b, matrix_c, counts, chunk)
-    sizes = lax.psum(jnp.sum(sums, axis=(1, 2)), ("gx", "gy", "gz"))
+    sizes = jnp.sum(sums, axis=(1, 2))
     step = target_ratio * jnp.sqrt(sizes[0] / (sizes[1] + epsilon))
     return finish(step[None], matrix_a, mixed, far_mixed, planes, twice, field, first)
 

time: 937 us -> 854 us (0.911)
  Pallas kernels: 884 us -> 841 us
  blocking collectives: 39.6 us -> 0 us
    pallas_call x1, Pallas kernels: 830 us -> 787 us  [pipeline(): pl.pallas_call(functools.partial(pipeline_kernel, counts, chunk), in_spec...]
    psum x1 -> x0, blocking collectives: 39.6 us -> none  [on_device(): sizes = lax.psum(jnp.sum(sums, axis=(1, 2)), ('gx', 'gy', 'gz'))]
where the time goes in v1:
time: 854 us; the launch traced here: 853 us
  Pallas kernels  841 us (98%)
    pallas_call x1, Pallas kernels, pipeline(): pl.pallas_call(functools.partial(pipeline_kernel, counts, chunk), in_spec...  787 us
    pallas_call x1, Pallas kernels, finish(): pl.pallas_call(functools.partial(finish_kernel, 1 + count), grid=(depth /...  53.5 us

profile of v1, /device:TPU:0, one launch (start us, length us, event | category | flops | bytes accessed | tf_op | source)
XLA Modules:
  0.0 852.8 jit_solution(858783605207140578)
XLA Ops:
  0.0 0.0 copy-start.1
  0.0 1.5 fusion.10
  1.5 0.1 fusion.8
  1.6 1.2 fusion.7
  2.8 0.3 fusion.6
  3.1 0.7 pad_maximum_fusion.3.matrix_c
  3.9 0.0 copy-done.1
  3.9 0.3 copy.5
  4.2 0.0 copy-start
  4.2 0.2 fusion.3
  4.4 1.1 pad_maximum_fusion.2.matrix_b
  5.5 1.3 copy-done
  6.8 0.6 dynamic-slice_bitcast_fusion.1
  7.4 0.4 reduce-precision_convert_fusion
  7.8 1.5 pad_maximum_fusion.1.matrix_a.matrix
  9.3 787.2 %pipeline.1 = (f32[64,512,128]{2,1,0:T(8,128)}, f32[64,512,128]{2,1,0:T(8,128)}, f32[64,512,128]{2,1,0:T(8,128)}, f32[2,64,512,128]{3,2,1,0:T(8,128)}, f32[1,64,...) custom-call(f32[64,512,128]{2,1,0:T(8,128)} %refs_4_.1, ...), custom_call_target="tpu_custom_call" | custom-call | tf_op jit(solution)/shard_map/pipeline/pallas_call | solution.py:538
  796.6 0.8 reduce_sum.9
  797.4 0.6 fusion.9
  799.3 53.5 %finish.1 = f32[64,512,128]{2,1,0:T(8,128)} custom-call(f32[1]{0:T(128)S(6)} %mul_shard_map.4.step, bf16[2,512,1024]{2,1,0:T(8,128)(2,1)} %pad_maximum_fusion.1.matrix_a.matrix, f32[64,512,128]{2,1,0:T(8,128)} %get-tuple-element.13.refs_0_, f32[1,64,512,128]{3,2,1,0:T(8,128)} %get-tuple-element.14.refs_1_, f32[2,64,512,128]{3,2,1,0:T(8,128)} %get-tuple-element.15.refs_2_, ...), custom_call_target="tpu_custom_call" | custom-call | tf_op jit(solution)/shard_map/finish/pallas_call | solution.py:583
  (1 shorter events, 0.0 us)
Async XLA Ops:
  0.0 3.9 copy-start.1
  4.2 2.6 copy-start

commit v2 on v1

--- a/solution.py
+++ b/solution.py
@@ -409,6 +409,16 @@
         sums[...] = total
 
     def tick_body(t, carry):
+        @pl.when(t < steps)
+        def _():
+            plane_start(field, t, t)
+
+        come = t - 2
+
+        @pl.when(valid(come))
+        def _():
+            plane_product(phase_of(come), chunk_of(come), come)
+
         for a in range(3):
 
             @pl.when(t == chunks + late + a)
@@ -430,10 +440,6 @@
         @pl.when(t + slots < chunks)
         def _():
             line_start(t + slots, False)
-
-        @pl.when(t < steps)
-        def _():
-            plane_start(field, t, t)
 
         ready = t - 4
 
@@ -448,12 +454,6 @@
             plane_start(mixed, c, t)
             for s in range(1, count_x):
                 far_mixed_copy(c, s).start()
-
-        come = t - 2
-
-        @pl.when(valid(come))
-        def _():
-            plane_product(phase_of(come), chunk_of(come), come)
 
         @pl.when(t == 1)
         def _():

time: 854 us -> 843 us (0.987)
  Pallas kernels: 841 us -> 829 us
    pallas_call x1, Pallas kernels: 787 us -> 776 us  [pipeline(): pl.pallas_call(functools.partial(pipeline_kernel, counts, chunk), in_spec...]
where the time goes in v2:
time: 843 us; the launch traced here: 841 us
  Pallas kernels  829 us (98%)
    pallas_call x1, Pallas kernels, pipeline(): pl.pallas_call(functools.partial(pipeline_kernel, counts, chunk), in_spec...  776 us
    pallas_call x1, Pallas kernels, finish(): pl.pallas_call(functools.partial(finish_kernel, 1 + count), grid=(depth /...  53.5 us

profile of v2, /device:TPU:0, one launch (start us, length us, event | category | flops | bytes accessed | tf_op | source)
XLA Modules:
  0.0 841.1 jit_solution(18003278737146632964)
XLA Ops:
  0.0 0.0 copy-start.1
  0.0 1.5 fusion.10
  1.5 0.1 fusion.8
  1.6 1.2 fusion.7
  2.8 0.3 fusion.6
  3.1 0.7 pad_maximum_fusion.3.matrix_c
  3.9 0.0 copy-done.1
  3.9 0.3 copy.5
  4.2 0.0 copy-start
  4.2 0.2 fusion.3
  4.4 1.1 pad_maximum_fusion.2.matrix_b
  5.5 1.3 copy-done
  6.8 0.6 dynamic-slice_bitcast_fusion.1
  7.4 0.4 reduce-precision_convert_fusion
  7.8 1.5 pad_maximum_fusion.1.matrix_a.matrix
  9.3 775.5 %pipeline.1 = (f32[64,512,128]{2,1,0:T(8,128)}, f32[64,512,128]{2,1,0:T(8,128)}, f32[64,512,128]{2,1,0:T(8,128)}, f32[2,64,512,128]{3,2,1,0:T(8,128)}, f32[1,64,...) custom-call(f32[64,512,128]{2,1,0:T(8,128)} %refs_4_.1, ...), custom_call_target="tpu_custom_call" | custom-call | tf_op jit(solution)/shard_map/pipeline/pallas_call | solution.py:538
  784.8 0.8 reduce_sum.9
  785.6 0.6 fusion.9
  787.5 53.5 %finish.1 = f32[64,512,128]{2,1,0:T(8,128)} custom-call(f32[1]{0:T(128)S(6)} %mul_shard_map.4.step, bf16[2,512,1024]{2,1,0:T(8,128)(2,1)} %pad_maximum_fusion.1.matrix_a.matrix, f32[64,512,128]{2,1,0:T(8,128)} %get-tuple-element.13.refs_0_, f32[1,64,512,128]{3,2,1,0:T(8,128)} %get-tuple-element.14.refs_1_, f32[2,64,512,128]{3,2,1,0:T(8,128)} %get-tuple-element.15.refs_2_, ...), custom_call_target="tpu_custom_call" | custom-call | tf_op jit(solution)/shard_map/finish/pallas_call | solution.py:583
  (1 shorter events, 0.0 us)
Async XLA Ops:
  0.0 3.9 copy-start.1
  4.2 2.6 copy-start
